TPU v7x, 32 devices: a whole 2x2x4 slice. The times are simulated.
32 devices in a mesh: rep: 2 (over x), data: 4 (over z), expert: 4 (over y, core).
Axes of the slice: x: 2, y: 2, z: 4, core: 2. Of those that a mesh axis runs over, the one named last changes fastest.
Arguments:
- x: bfloat16 [128, 512, 1024], P(('rep', 'expert', 'data')), parts along dimension 0
- expert_idx: int32 [128, 512, 8], P(('rep', 'expert', 'data')), parts along dimension 0
- gate: float32 [128, 512, 8], P(('rep', 'expert', 'data')), parts along dimension 0
- attn_gain: float32 [1024], replicated
- w_qkv: bfloat16 [1024, 32, 64], P(('data', 'expert'))
- w_out: bfloat16 [16, 64, 1024], P(None, None, ('data', 'expert'))
- moe_gain: float32 [1024], replicated
- w_gate: bfloat16 [32, 1024, 512], P('expert', 'data')
- w_up: bfloat16 [32, 1024, 512], P('expert', 'data')
- w_down: bfloat16 [32, 512, 1024], P('expert', None, 'data')
Outputs:
- output: bfloat16 [128, 512, 1024], P(('rep', 'expert', 'data')), parts along dimension 0
There are 2 independent parts. A program takes and returns all parts, laid end to end along the dimension named above; an argument that names none is the same for every part.
All inputs are finite; a program needn't handle non-finite values.
Results may differ from a plain program's by a relative error of at most 0.015028.
Values are sent between devices in bfloat16 or wider.
A program may use at most 1 GiB of HBM per device.

v0:
```python
import jax
import jax.numpy as jnp
from jax import lax
from jax.sharding import PartitionSpec as P

NORM_EPS = 1e-6
ROPE_BASE = 10000.0


def rms_scale(tok_rows, gain):
    rows_f32 = tok_rows.astype(jnp.float32)
    inv_rms = lax.rsqrt(jnp.mean(rows_f32 * rows_f32, axis=-1, keepdims=True) + NORM_EPS)
    return (rows_f32 * inv_rms * gain).astype(jnp.bfloat16)


def rope_apply(head_vals):
    seq_len, head_dim = head_vals.shape[1], head_vals.shape[-1]
    half_dim = head_dim // 2
    inv_freq = ROPE_BASE ** (-jnp.arange(half_dim, dtype=jnp.float32) * 2.0 / head_dim)
    angles = jnp.arange(seq_len, dtype=jnp.float32)[:, None] * inv_freq[None, :]
    cos_b = jnp.cos(angles)[None, :, None, :]
    sin_b = jnp.sin(angles)[None, :, None, :]
    vals_f32 = head_vals.astype(jnp.float32)
    low_half = vals_f32[..., :half_dim]
    high_half = vals_f32[..., half_dim:]
    return jnp.concatenate([low_half * cos_b - high_half * sin_b, high_half * cos_b + low_half * sin_b], axis=-1).astype(jnp.bfloat16)


def attention_block(seqs, attn_gain, w_qkv, w_out):
    num_seqs, seq_len, model_dim = seqs.shape
    head_dim = w_qkv.shape[2]
    num_heads = w_out.shape[0]
    kv_heads = (w_qkv.shape[1] - num_heads) // 2
    group_len = num_heads // kv_heads
    normed = rms_scale(seqs, attn_gain)
    qkv_all = jnp.einsum('uno,ojf->unjf', normed, w_qkv, preferred_element_type=jnp.float32).astype(jnp.bfloat16)
    queries = rope_apply(qkv_all[:, :, :num_heads]).reshape(num_seqs, seq_len, kv_heads, group_len, head_dim)
    keys_rot = rope_apply(qkv_all[:, :, num_heads:num_heads + kv_heads])
    values = qkv_all[:, :, num_heads + kv_heads:]
    scores = jnp.einsum('slkgd,smkd->skglm', queries, keys_rot, preferred_element_type=jnp.float32) * (head_dim ** -0.5)
    causal = lax.broadcasted_iota(jnp.int32, (seq_len, seq_len), 0) >= lax.broadcasted_iota(jnp.int32, (seq_len, seq_len), 1)
    attn_probs = jax.nn.softmax(jnp.where(causal, scores, -1e30), axis=-1).astype(jnp.bfloat16)
    mixed = jnp.einsum('skglm,smkd->slkgd', attn_probs, values, preferred_element_type=jnp.float32).astype(jnp.bfloat16)
    out_grouped = w_out.reshape(kv_heads, group_len, head_dim, model_dim)
    attn_proj = jnp.einsum('slkgd,kgdm->slm', mixed, out_grouped, preferred_element_type=jnp.float32)
    return (seqs.astype(jnp.float32) + attn_proj).astype(jnp.bfloat16)


def capacity_of(tok_dev, top_k, num_experts):
    return 8 * ((5 * top_k * tok_dev + 32 * num_experts - 1) // (32 * num_experts))


def dispatch_target(flat_ids, num_experts, capacity):
    onehot = (flat_ids[:, None] == jnp.arange(num_experts, dtype=jnp.int32)[None, :]).astype(jnp.int32)
    earlier = jnp.cumsum(onehot, axis=0) - onehot
    slot_pos = jnp.sum(earlier * onehot, axis=1)
    return jnp.where(slot_pos < capacity, flat_ids * capacity + slot_pos, num_experts * capacity)


def gather_rows(normed, target_rows, num_experts, capacity, top_k):
    tok_dev = normed.shape[0]
    source = jnp.full((num_experts * capacity + 1,), tok_dev, jnp.int32)
    source = source.at[target_rows].set(jnp.arange(tok_dev * top_k, dtype=jnp.int32) // top_k)
    padded = jnp.concatenate([normed, jnp.zeros((1, normed.shape[1]), normed.dtype)], axis=0)
    return jnp.take(padded, source[:num_experts * capacity], axis=0)


def combine_rows(expert_rows, target_rows, gate_rows):
    tok_dev, top_k = gate_rows.shape
    padded = jnp.concatenate([expert_rows, jnp.zeros((1, expert_rows.shape[1]), expert_rows.dtype)], axis=0)
    picked = jnp.take(padded, target_rows, axis=0).reshape(tok_dev, top_k, expert_rows.shape[1])
    return jnp.sum(picked.astype(jnp.float32) * gate_rows[:, :, None], axis=1)


def solution(mesh):
    expert_size = mesh.shape['expert']
    tok_spec = P(('rep', 'expert', 'data'), None, None)
    group_axes = ('data', 'expert')

    def local_step(x_loc, idx_loc, gate_loc, attn_gain, qkv_part, out_part, moe_gain, gate_part, up_part, down_part):
        w_qkv = lax.all_gather(qkv_part, group_axes, axis=0, tiled=True)
        w_out = lax.all_gather(out_part, group_axes, axis=2, tiled=True)
        hidden = attention_block(x_loc, attn_gain, w_qkv, w_out)
        num_seqs, seq_len, model_dim = hidden.shape
        tok_dev = num_seqs * seq_len
        top_k = idx_loc.shape[-1]
        loc_experts = gate_part.shape[0]
        num_experts = loc_experts * expert_size
        capacity = capacity_of(tok_dev, top_k, num_experts)
        flat_hidden = hidden.reshape(tok_dev, model_dim)
        normed = rms_scale(flat_hidden, moe_gain)
        target_rows = dispatch_target(idx_loc.reshape(tok_dev * top_k), num_experts, capacity)
        send_buf = gather_rows(normed, target_rows, num_experts, capacity, top_k).reshape(expert_size, loc_experts, capacity, model_dim)
        recv_buf = lax.all_to_all(send_buf, 'expert', 0, 2, tiled=True).reshape(loc_experts, expert_size * capacity, model_dim)
        w_gate = lax.all_gather(gate_part, 'data', axis=1, tiled=True)
        w_up = lax.all_gather(up_part, 'data', axis=1, tiled=True)
        w_down = lax.all_gather(down_part, 'data', axis=2, tiled=True)
        act_gate = jnp.einsum('ncm,nmf->ncf', recv_buf, w_gate, preferred_element_type=jnp.float32)
        act_up = jnp.einsum('ncm,nmf->ncf', recv_buf, w_up, preferred_element_type=jnp.float32)
        mid_act = (jax.nn.silu(act_gate) * act_up).astype(jnp.bfloat16)
        expert_out = jnp.einsum('ncf,nfm->ncm', mid_act, w_down, preferred_element_type=jnp.float32).astype(jnp.bfloat16)
        returned = lax.all_to_all(expert_out.reshape(1, loc_experts, expert_size * capacity, model_dim), 'expert', 2, 0, tiled=True)
        mixed_sum = combine_rows(returned.reshape(num_experts * capacity, model_dim), target_rows, gate_loc.reshape(tok_dev, top_k))
        total = flat_hidden.astype(jnp.float32) + mixed_sum
        return total.astype(jnp.bfloat16).reshape(num_seqs, seq_len, model_dim)

    in_specs = (tok_spec, tok_spec, tok_spec, P(None), P(group_axes, None, None), P(None, None, group_axes), P(None), P('expert', 'data', None), P('expert', 'data', None), P('expert', None, 'data'))
    return jax.shard_map(local_step, mesh=mesh, in_specs=in_specs, out_specs=tok_spec, check_vma=False)
```

profile of v0, /device:TPU:0, one launch (start us, length us, event | category | flops | bytes accessed | tf_op | source)
XLA Modules:
  0.0 1831.3 jit_solution(2646901787514559787)
XLA Ops:
  6.5 0.7 all-gather.6.cloned.1.call-update
  7.3 1.9 copy.28
  9.3 0.7 all-gather.10.cloned.1.call-update
  10.0 0.8 iota_compare_fusion.3
  10.8 1.2 copy.32
  11.9 0.5 eq.29
  12.4 0.5 eq.25
  12.9 0.8 broadcast_multiply_fusion
  13.8 3.1 fusion.7
  18.0 1.6 broadcast_add_fusion
  19.5 2.0 copy.35
  21.5 0.3 copy.37
  21.9 0.5 mul.249
  22.4 1.7 fusion.39
  24.3 60.8 %scatter_custom_fusion = s32[20481]{0:T(1024)S(1)} fusion(s32[16384]{0:T(1024)S(1)} %bitcast.135, s32[16384]{0:T(1024)S(1)} %add_select_fusion, s32[]{:T(128)} %constant.78.clone.1), kind=kCustom, calls=%fused_computation.81 | custom fusion | bytes 81928 | tf_op jit(solution)/shard_map/scatter | solution.py:63
  85.1 0.7 fusion.58
  85.8 0.6 compare_and_fusion.1
  86.5 0.4 all-gather.6.cloned.1.call-done
  86.8 9.7 copy.26
  96.6 12.4 convolution_convert_fusion
  109.0 1.2 slice_convert_fusion
  110.2 0.6 slice_convert_fusion.1
  110.8 1.7 copy-done
  112.5 2.8 subtract_convert_fusion
  115.3 1.8 subtract_convert_fusion.1
  117.0 30.9 %fusion.59 = (f32[4,8,2,512]{3,2,1,0:T(2,128)S(1)}, f32[4,8,2,512,512]{3,4,2,1,0:T(8,128)}) fusion(pred[512,512]{0,1:T(8,128)(4,1)S(1)} %copy-done.8, bf16[4,512,8,2,32]{1,4,3,2,0:T(8,128)(2,1)} %bitcast.132, bf16[4,512,8,2,32]{1,4,3,2,0:T(8,128)(2,1)S(1)} %bitcast.131, bf16[4,512,8,32]{1,3,2,0:T(8,128)(2,1)} %get-tuple-element.8, ...), kind=kOutput, calls=%fused_computation.95 | convolution fusion | flops 2227175936 | bytes 73793536 | tf_op jit(solution)/shard_map/sub | solution.py:42
  147.9 34.2 %multiply_reduce_fusion.1 = (f32[4,512]{1,0:T(4,128)S(1)}, f32[4,512,1024]{2,1,0:T(8,128)}) fusion(bf16[8,2,64,1024,1]{2,1,0,3,4:T(2,128)(2,1)} %bitcast.139, bf16[4,512,32,64]{1,3,2,0:T(8,128)(2,1)} %copy-done, bf16[4,512,1024]{2,1,0:T(8,128)(2,1)} %param.10, f32[4,8,2,512,512]{3,4,2,1,0:T(8,128)} %get-tuple-element.14, ...), kind=kOutput, calls=%fused_computation.29 | convolution fusion | flops 6490683392 | bytes 86122496 | tf_op jit(solution)/shard_map/slkgd,kgdm->slm/dot_general | solution.py:45
  182.2 3.9 fusion.12
  186.1 2.4 concatenate.23
  188.6 102.9 %gather_fusion = bf16[20480,1024]{1,0:T(8,128)(2,1)} fusion(bf16[2049,1024]{1,0:T(8,128)(2,1)} %concatenate.23, s32[20480]{0:T(1024)S(1)} %copy-done.5), kind=kCustom, calls=%fused_computation | custom fusion | bytes 83968000 | tf_op jit(solution)/shard_map/jit(_take)/gather | solution.py:65
  291.5 28.2 %broadcast_select_fusion = bf16[4,8,640,1024]{3,2,1,0:T(8,128)(2,1)} fusion(bf16[4,8,640,1024]{3,2,1,0:T(8,128)(2,1)} %bitcast.125, pred[4,8,640]{2,1,0:T(8,128)(4,1)S(1)} %copy-done.9), kind=kLoop, calls=%fused_computation.11 | loop fusion | flops 20971520 | bytes 83906560 | tf_op jit(solution)/shard_map/jit(_take)/select_n | solution.py:65
  319.6 11.2 all-to-all-start
  330.8 0.5 all-gather.12.cloned.1.call-update
  331.4 0.5 all-gather.14.cloned.1.call-update
  331.9 451.6 %all-to-all-done = bf16[4,8,640,1024]{3,2,1,0:T(8,128)(2,1)} async-done(((bf16[4,8,640,1024]{3,2,1,0:T(8,128)(2,1)}), bf16[4,8,640,1024]{3,2,1,0:T(8,128)(2,1)}, u32[]{:S(2)}, u32[]{:S(2)}) %all-to-all-start) | async-done | bytes 41943072 | tf_op jit(solution)/shard_map/all_to_all | solution.py:94
  783.5 28.6 %copy.38 = bf16[1,8,4,640,1024]{4,3,2,1,0:T(8,128)(2,1)} copy(bf16[1,8,4,640,1024]{4,3,1,2,0:T(8,128)(2,1)} %bitcast.23) | data formatting | bytes 83886080 | tf_op jit(solution)/shard_map/all_to_all | solution.py:94
  812.1 37.8 %fusion.62 = f32[8,2560,512]{2,1,0:T(8,128)} fusion(bf16[8,2560,1024]{2,1,0:T(8,128)(2,1)} %bitcast.127, bf16[8,1024,512]{2,1,0:T(8,128)(2,1)} %all-gather.10.cloned.1.call-done), kind=kOutput, calls=%fused_computation.96 | convolution fusion | flops 21474836480 | bytes 92274688 | tf_op jit(solution)/shard_map/ncm,nmf->ncf/dot_general | solution.py:98
  849.9 60.0 %convert_bitcast_fusion = bf16[1,8,2560,1024]{3,2,1,0:T(8,128)(2,1)} fusion(bf16[8,512,1024]{2,1,0:T(8,128)(2,1)} %all-gather.14.cloned.1.call-done, f32[8,2560,512]{2,1,0:T(8,128)} %fusion.62, bf16[8,2560,1024]{2,1,0:T(8,128)(2,1)} %bitcast.128, bf16[8,1024,512]{2,1,0:T(8,128)(2,1)} %all-gather.12.cloned.1.call-done), kind=kOutput, calls=%fused_computation.9 | convolution fusion | flops 43033559040 | bytes 142606336 | tf_op jit(solution)/shard_map/ncf,nfm->ncm/dot_general | solution.py:101
  909.9 37.8 %copy.39 = bf16[1,8,2560,1024]{3,1,0,2:T(8,128)(2,1)} copy(bf16[1,8,2560,1024]{3,2,1,0:T(8,128)(2,1)} %convert_bitcast_fusion) | data formatting | bytes 83886080 | tf_op jit(solution)/shard_map/reshape | solution.py:102
  947.7 11.6 all-to-all-start.1
  959.3 0.6 reduce_sum.54
  960.6 0.4 compare_and_fusion
  961.1 450.6 %all-to-all-done.1 = bf16[1,8,2560,1024]{3,1,0,2:T(8,128)(2,1)} async-done(((bf16[1,8,2560,1024]{3,1,0,2:T(8,128)(2,1)}), bf16[1,8,2560,1024]{3,1,0,2:T(8,128)(2,1)}, u32[]{:S(2)}, u32[]{:S(2)}) %all-to-all-start.1) | async-done | bytes 41943072 | tf_op jit(solution)/shard_map/all_to_all | solution.py:102
  1411.7 37.8 %copy.40 = bf16[1,8,4,640,1024]{4,3,1,2,0:T(8,128)(2,1)} copy(bf16[1,8,4,640,1024]{4,1,3,2,0:T(8,128)(2,1)} %bitcast.26) | data formatting | bytes 83886080 | tf_op jit(solution)/shard_map/all_to_all | solution.py:102
  1449.5 28.6 %concatenate.24 = bf16[20481,1024]{1,0:T(8,128)(2,1)} pad(bf16[20480,1024]{1,0:T(8,128)(2,1)} %bitcast.126, bf16[]{:T(256)} %constant.84.clone.1), padding=0_1x0_0 | pad | bytes 83888128 | tf_op jit(solution)/shard_map/concatenate | solution.py:70
  1478.0 302.2 %gather_fusion.1 = bf16[16384,1024]{1,0:T(8,128)(2,1)} fusion(bf16[20481,1024]{1,0:T(8,128)(2,1)} %concatenate.24, s32[16384]{0:T(1024)S(1)} %broadcast_clamp_fusion), kind=kCustom, calls=%fused_computation.1 | custom fusion | bytes 67174400 | tf_op jit(solution)/shard_map/jit(_take)/gather | solution.py:71
  1780.3 34.8 %multiply_reduce_fusion = f32[2048,1024]{1,0:T(8,128)} fusion(bf16[16384,1024]{1,0:T(8,128)(2,1)} %gather_fusion.1, f32[2048,8]{1,0:T(8,128)S(1)} %copy.41, pred[2048,8]{1,0:T(8,128)(4,1)S(1)} %compare_and_fusion), kind=kLoop, calls=%fused_computation.5 | loop fusion | flops 65011712 | bytes 42024960 | tf_op jit(solution)/shard_map/reduce_sum | solution.py:72
  1815.0 9.3 add_convert_fusion
  (51 shorter events, 2.1 us)
Async XLA Ops:
  6.5 80.3 %all-gather.6.cloned.1.call-start = ((), (), s32[]{:S(2)}) async-start(), calls=%async_computation.2 | async-start | bytes 8912896 | tf_op jit(solution)/shard_map/all_gather | solution.py:81
  7.3 140.7 %all-gather.8.cloned.1.call-start = ((), (), s32[]{:S(2)}) async-start(), calls=%async_computation.3 | async-start | bytes 4456448 | tf_op jit(solution)/shard_map/all_gather | solution.py:82
  9.2 802.9 %all-gather.10.cloned.1.call-start = ((), (), s32[]{:S(2)}) async-start(), calls=%async_computation.4 | async-start | bytes 10485760 | tf_op jit(solution)/shard_map/all_gather | solution.py:95
  13.8 8.6 copy-start.3
  21.9 74.7 %copy-start.12 = (f32[1024]{0:T(1024)S(1)}, f32[1024]{0:T(1024)}, u32[]{:S(2)}) copy-start(f32[1024]{0:T(1024)} %param.13) | copy-start | bytes 12292
  24.2 84.8 %copy-start.1 = (s32[16384]{0:T(1024)}, s32[16384]{0:T(1024)S(1)}, u32[]{:S(2)}) copy-start(s32[16384]{0:T(1024)S(1)} %fusion.39) | copy-start | bytes 196612
  24.3 84.7 %copy-start.6 = (s32[16384,1]{0,1:T(1,128)}, s32[16384,1]{0,1:T(1,128)S(1)}, u32[]{:S(2)}) copy-start(s32[16384,1]{0,1:T(1,128)S(1)} %compare_select_fusion.1) | copy-start | bytes 196612
  109.0 3.5 copy-start
  112.5 4.5 copy-start.8
  147.9 34.2 %copy-start.11 = (f32[1024]{0:T(1024)S(1)}, f32[1024]{0:T(1024)}, u32[]{:S(2)}) copy-start(f32[1024]{0:T(1024)} %param.16) | copy-start | bytes 12292
  182.2 6.4 copy-start.5
  188.6 102.9 %copy-start.9 = (pred[4,8,640]{2,1,0:T(8,128)(4,1)S(1)}, pred[4,8,640]{2,1,0:T(8,128)(4,1)}, u32[]{:S(2)}) copy-start(pred[4,8,640]{2,1,0:T(8,128)(4,1)} %compare_and_fusion.1) | copy-start | bytes 61444
  319.6 463.9 %all-to-all-start = ((bf16[4,8,640,1024]{3,2,1,0:T(8,128)(2,1)}), bf16[4,8,640,1024]{3,2,1,0:T(8,128)(2,1)}, u32[]{:S(2)}, u32[]{:S(2)}) async-start(bf16[4,8,640,1024]{3,2,1,0:T(8,128)(2,1)} %broadcast_select_fusion), calls=%async_computation | async-start | bytes 83886080 | tf_op jit(solution)/shard_map/all_to_all | solution.py:94
  330.8 519.1 %all-gather.12.cloned.1.call-start = ((), (), s32[]{:S(2)}) async-start(), calls=%async_computation.5 | async-start | bytes 10485760 | tf_op jit(solution)/shard_map/all_gather | solution.py:96
  331.4 518.6 %all-gather.14.cloned.1.call-start = ((), (), s32[]{:S(2)}) async-start(), calls=%async_computation.6 | async-start | bytes 10485760 | tf_op jit(solution)/shard_map/all_gather | solution.py:97
  947.7 11.6 copy-start.2
  947.7 12.2 copy-start.4
  947.7 12.6 copy-start.10
  947.7 12.9 copy-start.7
  947.7 464.0 %all-to-all-start.1 = ((bf16[1,8,2560,1024]{3,1,0,2:T(8,128)(2,1)}), bf16[1,8,2560,1024]{3,1,0,2:T(8,128)(2,1)}, u32[]{:S(2)}, u32[]{:S(2)}) async-start(bf16[1,8,2560,1024]{3,1,0,2:T(8,128)(2,1)} %copy.39), calls=%async_computation.1 | async-start | bytes 83886080 | tf_op jit(solution)/shard_map/all_to_all | solution.py:102
Sparse Core Ops, SparseCore 0:
  9.5 77.2 all-gather.5
  89.0 48.6 all-gather.7
  139.3 148.3 all-gather.9
  332.8 152.3 all-gather.11
  486.6 148.5 all-gather.13
where the time goes:
time: 1840 us; the launch traced here: 1830 us
  waiting for transfers between devices  905 us (49%)
  local copies, waits for them, and re-layouts  621 us (34%)
  matrix products  175 us (10%)
  other arithmetic  93.2 us (5%)
  starting transfers between devices  22.9 us (1%)
    all_to_all x1, waiting for transfers between devices, local_step(): lax.all_to_all(send_buf, 'expert', 0, 2, tiled=True)  452 us
    all_to_all x1, waiting for transfers between devices, local_step(): lax.all_to_all(expert_out.reshape(1, loc_experts, expert_size * capacity,...  451 us
    gather x1, local copies, waits for them, and re-layouts, combine_rows(): jnp.take(padded, target_rows, axis=0)  302 us
    gather x1, local copies, waits for them, and re-layouts, gather_rows(): return jnp.take(padded, source[:num_experts * capacity], axis=0)  103 us
    scatter x1, local copies, waits for them, and re-layouts, gather_rows(): source.at[target_rows]  60.8 us
    dot_general x1, matrix products, local_step(): jnp.einsum('ncf,nfm->ncm', mid_act, w_down, preferred_element_type=jnp.fl...  60 us
    dot_general x1, matrix products, local_step(): jnp.einsum('ncm,nmf->ncf', recv_buf, w_gate, preferred_element_type=jnp.f...  37.8 us
    all_to_all x1, local copies, waits for them, and re-layouts, local_step(): lax.all_to_all(expert_out.reshape(1, loc_experts, expert_size * capacity,...  37.8 us
  transfers between devices with their start and end apart: 7, of which 3 were waited for; matrix products, arithmetic and copies ran while one was open for 21% of the time, Pallas kernels for 0%

commit v1 on v0

v1 whole, which is shorter than its diff:
```python
import functools

import jax
import jax.numpy as jnp
from jax import lax
from jax.experimental import pallas as pl
from jax.experimental.pallas import tpu as pltpu
from jax.sharding import PartitionSpec as P

NORM_EPS = 1e-6
ROPE_BASE = 10000.0
LANES = 128
VMEM_LIMIT = 64000 * 1024


def capacity_of(tok_dev, top_k, num_experts):
    return 8 * ((5 * top_k * tok_dev + 32 * num_experts - 1) // (32 * num_experts))


def rope_tables(seq_len, head_dim):
    half_dim = head_dim // 2
    inv_freq = ROPE_BASE ** (-jnp.arange(half_dim, dtype=jnp.float32) * 2.0 / head_dim)
    angles = jnp.arange(seq_len, dtype=jnp.float32)[:, None] * inv_freq[None, :]
    cos_b, sin_b = jnp.cos(angles), jnp.sin(angles)
    return jnp.concatenate([cos_b] * 4, axis=1), jnp.concatenate([-sin_b, sin_b] * 2, axis=1)


def route_kernel(capacity, idx_ref, gate_ref, tok_ref, gates_ref, count_ref, slot_scr):
    top_k, tokens = idx_ref.shape
    experts = gates_ref.shape[0]
    expert_id = lax.broadcasted_iota(jnp.int32, (experts, tokens), 0)
    chosen = jnp.zeros((experts, tokens), jnp.float32)
    gates = jnp.zeros((experts, tokens), jnp.float32)
    for k in range(top_k):
        hit = idx_ref[k:k + 1, :] == expert_id
        chosen = chosen + jnp.where(hit, 1.0, 0.0)
        gates = gates + jnp.where(hit, gate_ref[k:k + 1, :], 0.0)
    gates_ref[...] = gates
    blk = 256
    upper = jnp.where(lax.broadcasted_iota(jnp.int32, (blk, blk), 0) < lax.broadcasted_iota(jnp.int32, (blk, blk), 1), 1.0, 0.0).astype(jnp.bfloat16)
    before = jnp.zeros((experts, 1), jnp.float32)
    for b in range(tokens // blk):
        part = chosen[:, b * blk:(b + 1) * blk]
        earlier = jnp.dot(part.astype(jnp.bfloat16), upper, preferred_element_type=jnp.float32) + before
        slot = jnp.where((part > 0.0) & (earlier < capacity), earlier, -1.0)
        slot_scr[:, b * blk:(b + 1) * blk] = slot.astype(jnp.int32)
        before = before + jnp.sum(part, axis=1, keepdims=True)
    count_ref[...] = jnp.broadcast_to(jnp.minimum(before, float(capacity)), count_ref.shape).astype(jnp.int32)
    tok_id = lax.broadcasted_iota(jnp.int32, (8, tokens), 1)
    tok_hi = (tok_id >> 8).astype(jnp.float32)
    tok_lo = (tok_id & 255).astype(jnp.float32)
    row_id = lax.broadcasted_iota(jnp.int32, (8, tokens), 0)
    lane_id = lax.broadcasted_iota(jnp.int32, (LANES, tokens), 0)

    def one(e, carry):
        slot = slot_scr[pl.ds(e, 1), :]
        major = jnp.broadcast_to(slot >> 7, (8, tokens)) == row_id
        left = jnp.concatenate([jnp.where(major, tok_hi, 0.0), jnp.where(major, tok_lo, 0.0)], axis=0).astype(jnp.bfloat16)
        minor = jnp.where((slot & 127) == lane_id, 1.0, 0.0).astype(jnp.bfloat16)
        found = lax.dot_general(left, minor, (((1,), (1,)), ((), ())), preferred_element_type=jnp.float32)
        tok_ref[pl.ds(e, 1)] = ((found[:8] * 256.0 + found[8:]) * 8.0).astype(jnp.int32).reshape(1, 8, LANES)
        return carry

    lax.fori_loop(0, experts, one, 0)


def route(idx_t, gate_t, num_experts, capacity):
    tokens = idx_t.shape[1]
    return pl.pallas_call(
        functools.partial(route_kernel, capacity),
        out_shape=(
            jax.ShapeDtypeStruct((num_experts, 8, LANES), jnp.int32),
            jax.ShapeDtypeStruct((num_experts, tokens), jnp.float32),
            jax.ShapeDtypeStruct((num_experts, LANES), jnp.int32),
        ),
        scratch_shapes=[pltpu.VMEM((num_experts, tokens), jnp.int32)],
        compiler_params=pltpu.CompilerParams(vmem_limit_bytes=VMEM_LIMIT),
        cost_estimate=pl.CostEstimate(flops=10_000_000_000, bytes_accessed=1_000_000, transcendentals=0),
        name="route",
    )(idx_t, gate_t)


def rms(rows_f32, gain):
    inv = lax.rsqrt(jnp.mean(rows_f32 * rows_f32, axis=-1, keepdims=True) + NORM_EPS)
    return (rows_f32 * inv * gain).astype(jnp.bfloat16)


def attn_kernel(x_ref, ag_ref, wqkv_ref, wout_ref, mg_ref, cos_ref, sin_ref, h_ref, z_ref, u_scr, qkv_scr, mix_scr):
    seq, dim = x_ref.shape[1], x_ref.shape[2]
    rb = 256
    for r in range(0, seq, rb):
        u_scr[r:r + rb, :] = rms(x_ref[0, r:r + rb, :].astype(jnp.float32), ag_ref[...])
    nq = dim // LANES
    nk = nq // 2
    nblk = 512

    def proj(n, carry):
        cols = pl.ds(pl.multiple_of(n * nblk, nblk), nblk)
        qkv_scr[:, cols] = jnp.dot(u_scr[...], wqkv_ref[:, cols], preferred_element_type=jnp.float32).astype(jnp.bfloat16)
        return carry

    lax.fori_loop(0, qkv_scr.shape[1] // nblk, proj, 0)
    lane = lax.broadcasted_iota(jnp.int32, (seq, LANES), 1)
    low = (lane & 63) < 32
    left = lane < 64
    left_rb = left[:rb]

    def rope(v):
        partner = jnp.where(low, pltpu.roll(v, LANES - 32, 1), pltpu.roll(v, 32, 1))
        return v * cos_ref[...] + partner * sin_ref[...]

    causal = lax.broadcasted_iota(jnp.int32, (rb, rb), 0) >= lax.broadcasted_iota(jnp.int32, (rb, rb), 1)

    def pair(p, carry):
        kcol = pl.ds(pl.multiple_of(dim + p * LANES, LANES), LANES)
        vcol = pl.ds(pl.multiple_of(dim + nk * LANES + p * LANES, LANES), LANES)
        keys = rope(qkv_scr[:, kcol].astype(jnp.float32))
        keys_sw = pltpu.roll(keys, 64, 1)
        vals = qkv_scr[:, vcol].astype(jnp.float32)
        vals_sw = pltpu.roll(vals, 64, 1)
        for j in range(2):
            first, second = (keys, keys_sw) if j == 0 else (keys_sw, keys)
            kk = jnp.where(left, first, second).astype(jnp.bfloat16)
            first, second = (vals, vals_sw) if j == 0 else (vals_sw, vals)
            vv = jnp.where(left, first, second).astype(jnp.bfloat16)
            qcol = pl.ds(pl.multiple_of((2 * p + j) * LANES, LANES), LANES)
            q = rope(qkv_scr[:, qcol].astype(jnp.float32)) * 0.125
            for r in range(0, seq, rb):
                qr = q[r:r + rb]
                outs = []
                for half in range(2):
                    qh = jnp.where(left_rb if half == 0 else ~left_rb, qr, 0.0).astype(jnp.bfloat16)
                    s = lax.dot_general(qh, kk[:r + rb], (((1,), (1,)), ((), ())), preferred_element_type=jnp.float32)
                    diag = jnp.where(causal, s[:, r:], -1e30)
                    s = diag if r == 0 else jnp.concatenate([s[:, :r], diag], axis=1)
                    e = jnp.exp(s - jnp.max(s, axis=1, keepdims=True))
                    probs = (e * (1.0 / jnp.sum(e, axis=1, keepdims=True))).astype(jnp.bfloat16)
                    outs.append(jnp.dot(probs, vv[:r + rb], preferred_element_type=jnp.float32))
                mix_scr[r:r + rb, qcol] = jnp.where(left_rb, outs[0], outs[1]).astype(jnp.bfloat16)
        return carry

    lax.fori_loop(0, nk, pair, 0)
    for r in range(0, seq, rb):
        proj_out = jnp.dot(mix_scr[r:r + rb, :], wout_ref[...], preferred_element_type=jnp.float32)
        hid = (x_ref[0, r:r + rb, :].astype(jnp.float32) + proj_out).astype(jnp.bfloat16).astype(jnp.float32)
        normed = rms(hid, mg_ref[...]).astype(jnp.float32)
        for c in range(dim // LANES):
            rows = pl.ds(r * 8 + c, rb, stride=8)
            h_ref[rows, :] = hid[:, c * LANES:(c + 1) * LANES]
            z_ref[rows, :] = normed[:, c * LANES:(c + 1) * LANES]


def attention(x, attn_gain, w_qkv, w_out, moe_gain):
    num, seq, dim = x.shape
    cos_t, sin_t = rope_tables(seq, 64)
    whole = lambda *shape: pl.BlockSpec(shape, lambda s: (0,) * len(shape), pipeline_mode=pl.Buffered(1))
    rows_out = jax.ShapeDtypeStruct((num * seq * 8, LANES), jnp.float32)
    return pl.pallas_call(
        attn_kernel,
        grid=(num,),
        in_specs=[pl.BlockSpec((1, seq, dim), lambda s: (s, 0, 0)), whole(1, dim), whole(dim, 2 * dim), whole(dim, dim), whole(1, dim), whole(seq, LANES), whole(seq, LANES)],
        out_specs=[pl.BlockSpec((seq * 8, LANES), lambda s: (s, 0))] * 2,
        out_shape=(rows_out, rows_out),
        scratch_shapes=[pltpu.VMEM((seq, dim), jnp.bfloat16), pltpu.VMEM((seq, 2 * dim), jnp.bfloat16), pltpu.VMEM((seq, dim), jnp.bfloat16)],
        compiler_params=pltpu.CompilerParams(vmem_limit_bytes=VMEM_LIMIT),
        cost_estimate=pl.CostEstimate(flops=60_000_000_000, bytes_accessed=30_000_000, transcendentals=0),
        name="attention",
    )(x, attn_gain.reshape(1, dim), w_qkv, w_out, moe_gain.reshape(1, dim), cos_t, sin_t)


def expert_kernel(last, capacity, ids_ref, count_ref, tok_ref, gates_ref, z_hbm, acc_hbm, w_ref, out_ref, z_scr, acc_scr, rows_scr, in_scr, sem):
    step = pl.program_id(0)
    dim = in_scr.shape[1]
    chunks = dim // LANES

    @pl.when(step == 0)
    def _():
        cz = pltpu.make_async_copy(z_hbm, z_scr, sem.at[0])
        ca = pltpu.make_async_copy(acc_hbm, acc_scr, sem.at[1])
        cz.start()
        ca.start()
        cz.wait()
        ca.wait()

    count = count_ref[ids_ref[step]]
    unroll = 16
    trips = (count + unroll - 1) // unroll

    def take(i, carry):
        base = i * unroll
        for j in range(unroll):
            src = pl.multiple_of(tok_ref[0, 0, base + j], 8)
            rows_scr[pl.ds(pl.multiple_of((base + j) * 8, 8), 8), :] = z_scr[pl.ds(src, 8), :]
        return carry

    lax.fori_loop(0, trips, take, 0)
    for c in range(chunks):
        in_scr[:, c * LANES:(c + 1) * LANES] = rows_scr[pl.ds(c, capacity, stride=8), :].astype(jnp.bfloat16)
    rb = 320
    quarter = w_ref.shape[4]
    for r in range(0, capacity, rb):
        act_g = None
        for q in range(4):
            xq = in_scr[r:r + rb, q * quarter:(q + 1) * quarter]
            pg = jnp.dot(xq, w_ref[0, 0, q, 0], preferred_element_type=jnp.float32)
            pu = jnp.dot(xq, w_ref[0, 0, q, 1], preferred_element_type=jnp.float32)
            act_g, act_u = (pg, pu) if act_g is None else (act_g + pg, act_u + pu)
        mid = (act_g * jax.nn.sigmoid(act_g) * act_u).astype(jnp.bfloat16)
        for q in range(4):
            down = w_ref[0, 0, q, 2]
            o = jnp.dot(mid[:, :quarter], down[:, :quarter], preferred_element_type=jnp.float32) + jnp.dot(mid[:, quarter:], down[:, quarter:], preferred_element_type=jnp.float32)
            o = o.astype(jnp.bfloat16).astype(jnp.float32)
            for c in range(quarter // LANES):
                rows_scr[pl.ds(r * 8 + q * (quarter // LANES) + c, rb, stride=8), :] = o[:, c * LANES:(c + 1) * LANES]

    def put(i, carry):
        base = i * unroll
        spots, sums = [], []
        for j in range(unroll):
            dst = pl.multiple_of(tok_ref[0, 0, base + j], 8)
            gate = gates_ref[0, 0, dst >> 3]
            spots.append(pl.ds(dst, 8))
            sums.append(acc_scr[spots[-1], :] + gate * rows_scr[pl.ds(pl.multiple_of((base + j) * 8, 8), 8), :])
        for j in range(unroll):
            acc_scr[spots[j], :] = sums[j]
        return carry

    full = count // unroll
    lax.fori_loop(0, full, put, 0)

    def put_one(i, carry):
        dst = pl.multiple_of(tok_ref[0, 0, i], 8)
        acc_scr[pl.ds(dst, 8), :] = acc_scr[pl.ds(dst, 8), :] + gates_ref[0, 0, dst >> 3] * rows_scr[pl.ds(pl.multiple_of(i * 8, 8), 8), :]
        return carry

    lax.fori_loop(full * unroll, count, put_one, 0)

    @pl.when(step == pl.num_programs(0) - 1)
    def _():
        if last:
            tokens = out_ref.shape[0]
            tb = 512
            for t in range(0, tokens, tb):
                for c in range(chunks):
                    out_ref[t:t + tb, c * LANES:(c + 1) * LANES] = acc_scr[pl.ds(t * 8 + c, tb, stride=8), :].astype(jnp.bfloat16)
        else:
            co = pltpu.make_async_copy(acc_scr, out_ref, sem.at[0])
            co.start()
            co.wait()


def experts(ids, count, tok, gates, z, acc, w, capacity, last):
    steps = ids.shape[0]
    tokens = gates.shape[2]
    dim = 8 * LANES
    if last:
        out_shape, out_spec = jax.ShapeDtypeStruct((tokens, dim), jnp.bfloat16), pl.BlockSpec((tokens, dim), lambda s, i, n: (0, 0), pipeline_mode=pl.Buffered(1))
    else:
        out_shape, out_spec = jax.ShapeDtypeStruct(acc.shape, jnp.float32), pl.BlockSpec(memory_space=pl.ANY)
    n_pos = w.shape[1]
    grid_spec = pltpu.PrefetchScalarGridSpec(
        num_scalar_prefetch=2,
        grid=(steps,),
        in_specs=[
            pl.BlockSpec((1, 1, tok.shape[2]), lambda s, i, n: (i[s], 0, 0), memory_space=pltpu.SMEM),
            pl.BlockSpec((1, 1, tokens), lambda s, i, n: (i[s], 0, 0), memory_space=pltpu.SMEM),
            pl.BlockSpec(memory_space=pl.ANY),
            pl.BlockSpec(memory_space=pl.ANY),
            pl.BlockSpec((1, 1) + w.shape[2:], lambda s, i, n: (s // n_pos, s % n_pos, 0, 0, 0, 0)),
        ],
        out_specs=out_spec,
        scratch_shapes=[
            pltpu.VMEM((tokens * 8, LANES), jnp.float32),
            pltpu.VMEM((tokens * 8, LANES), jnp.float32),
            pltpu.VMEM((capacity * 8, LANES), jnp.float32),
            pltpu.VMEM((capacity, dim), jnp.bfloat16),
            pltpu.SemaphoreType.DMA((2,)),
        ],
    )
    return pl.pallas_call(
        functools.partial(expert_kernel, last, capacity),
        grid_spec=grid_spec,
        out_shape=out_shape,
        input_output_aliases={} if last else {5: 0},
        compiler_params=pltpu.CompilerParams(vmem_limit_bytes=VMEM_LIMIT),
        cost_estimate=pl.CostEstimate(flops=5_000_000_000 * steps, bytes_accessed=3_500_000 * steps, transcendentals=0),
        name="experts",
    )(ids, count, tok, gates, z, acc, w)


def pack(gate_part, up_part, down_part):
    half = down_part.shape[1] // 2
    down = jnp.concatenate([down_part[:, :half], down_part[:, half:]], axis=2)
    return jnp.stack([gate_part, up_part, down], axis=1)


def solution(mesh):
    tok_spec = P(('rep', 'expert', 'data'), None, None)
    group_axes = ('data', 'expert')
    n_exp, n_rep = mesh.shape['expert'], mesh.shape['rep']

    def local_step(x, idx, gate, attn_gain, qkv_part, out_part, moe_gain, gate_part, up_part, down_part):
        num_seqs, seq_len, dim = x.shape
        tokens = num_seqs * seq_len
        top_k = idx.shape[-1]
        loc = gate_part.shape[0]
        num_experts = loc * n_exp
        capacity = capacity_of(tokens, top_k, num_experts)
        w_qkv = lax.all_gather(qkv_part.reshape(qkv_part.shape[0], -1), group_axes, axis=0, tiled=True)
        w_out = lax.all_gather(out_part.reshape(-1, out_part.shape[2]), group_axes, axis=1, tiled=True)
        rep = lax.axis_index('rep')
        packed = pack(gate_part, up_part, down_part)
        chunks = loc // n_rep
        gathered = []
        for c in range(chunks):
            mine = lax.dynamic_index_in_dim(packed, c * n_rep + rep, 0, keepdims=False)
            whole = lax.all_gather(mine, ('rep', 'expert', 'data'), axis=0, tiled=False)
            gathered.append(whole.reshape((n_rep, n_exp, mesh.shape['data']) + mine.shape))
        tok, gates, count = route(idx.reshape(tokens, top_k).T, gate.reshape(tokens, top_k).T, num_experts, capacity)
        tok = tok.reshape(num_experts, 1, 8 * LANES)
        gates = gates.reshape(num_experts, 1, tokens)
        count = count[:, 0]
        acc, z = attention(x, attn_gain, w_qkv, w_out, moe_gain)
        for c in range(chunks):
            ids = jnp.asarray([e * loc + c * n_rep + r for r in range(n_rep) for e in range(n_exp)], jnp.int32)
            acc = experts(ids, count, tok, gates, z, acc, gathered[c], capacity, c == chunks - 1)
        return acc.reshape(num_seqs, seq_len, dim)

    in_specs = (tok_spec, tok_spec, tok_spec, P(None), P(group_axes, None, None), P(None, None, group_axes), P(None), P('expert', 'data', None), P('expert', 'data', None), P('expert', None, 'data'))
    return jax.shard_map(local_step, mesh=mesh, in_specs=in_specs, out_specs=tok_spec, check_vma=False)
```

time: 1840 us -> 808 us (0.44)
  local copies, waits for them, and re-layouts: 621 us -> 97 us
  waiting for transfers between devices: 905 us -> 413 us
  Pallas kernels: 0 us -> 281 us
  matrix products: 175 us -> 0 us
  other arithmetic: 93.2 us -> 3.29 us
  starting transfers between devices: 22.9 us -> 0.2 us
    all_to_all x2 -> x0, waiting for transfers between devices: 902 us -> none  [the longest x1 452 us: local_step(): lax.all_to_all(send_buf, 'expert', 0, 2, tiled=True)]
    all_gather x5 -> x6, waiting for transfers between devices: 0.38 us -> 411 us  [the longest x4 343 us: local_step(): whole = lax.all_gather(mine, ('rep', 'expert', 'data'), axis=0, tiled=False)]
    gather x2 -> x0, local copies, waits for them, and re-layouts: 405 us -> none  [the longest x1 302 us: combine_rows(): jnp.take(padded, target_rows, axis=0)]
    pallas_call x0 -> x6, Pallas kernels: none -> 281 us  [the longest x4 190 us: experts(): pl.pallas_call(functools.partial(expert_kernel, last, capacity), grid_spe...]
    dot_general x4 -> x0, matrix products: 144 us -> none  [the longest x1 60 us: local_step(): jnp.einsum('ncf,nfm->ncm', mid_act, w_down, preferred_element_type=jnp.fl...]
    all_gather x1 -> x5, local copies, waits for them, and re-layouts: 9.74 us -> 85.9 us  [the longest x4 81.9 us: local_step(): whole = lax.all_gather(mine, ('rep', 'expert', 'data'), axis=0, tiled=False)]
    all_to_all x2 -> x0, local copies, waits for them, and re-layouts: 66.4 us -> none  [the longest x1 37.8 us: local_step(): lax.all_to_all(expert_out.reshape(1, loc_experts, expert_size * capacity,...]
    scatter x1 -> x0, local copies, waits for them, and re-layouts: 60.8 us -> none  [gather_rows(): source.at[target_rows]]
  transfers between devices with their start and end apart: 7 -> 6, of which waited for: 3 -> 5; matrix products, arithmetic and copies ran while one was open for 21% -> 10% of each run, Pallas kernels for 0% -> 29%
where the time goes in v1:
time: 808 us
  waiting for transfers between devices  413 us (51%)
  Pallas kernels  281 us (35%)
  local copies, waits for them, and re-layouts  97 us (12%)
  between operations  13.6 us (2%)
    all_gather x4, waiting for transfers between devices, local_step(): whole = lax.all_gather(mine, ('rep', 'expert', 'data'), axis=0, tiled=False)  343 us
    pallas_call x4, Pallas kernels, experts(): pl.pallas_call(functools.partial(expert_kernel, last, capacity), grid_spe...  190 us
    all_gather x4, local copies, waits for them, and re-layouts, local_step(): whole = lax.all_gather(mine, ('rep', 'expert', 'data'), axis=0, tiled=False)  81.9 us
    pallas_call x1, Pallas kernels, attention(): pl.pallas_call(attn_kernel, grid=(num,), in_specs=[pl.BlockSpec((1, seq,...  80.5 us
    all_gather x1, waiting for transfers between devices, local_step(): lax.all_gather(qkv_part.reshape(qkv_part.shape[0], -1), group_axes, axis=...  47.3 us
    all_gather x1, waiting for transfers between devices, local_step(): lax.all_gather(out_part.reshape(-1, out_part.shape[2]), group_axes, axis=...  20.6 us
  transfers between devices with their start and end apart: 6, of which 5 were waited for; matrix products, arithmetic and copies ran while one was open for 10% of the time, Pallas kernels for 29%

profile of v1, /device:TPU:0, one launch (start us, length us, event | category | flops | bytes accessed | tf_op | source)
XLA Modules:
  0.0 807.8 jit_solution(10208262152943777249)
XLA Ops:
  6.5 0.0 copy-start
  6.5 0.0 all-gather.9.cloned.1.call-start
  6.5 1.9 copy.32
  8.4 0.0 all-gather.9.cloned.1.call-update
  8.4 0.0 all-gather.7.cloned.1.call-start
  8.5 2.2 reshape.50
  10.7 0.0 all-gather.7.cloned.1.call-update
  10.7 0.0 all-gather.11.cloned.1.call-start
  10.8 0.0 copy-start.1
  10.8 1.9 fusion.3
  12.7 0.2 maximum_bitcast_fusion
  12.9 0.0 copy-done
  12.9 0.1 copy-done.1
  13.0 0.8 pad_maximum_fusion
  13.9 1.8 constant_dynamic-slice_fusion
  15.7 0.0 all-gather.11.cloned.1.call-update
  15.7 0.0 all-gather.13.cloned.1.call-start
  15.7 0.5 all-gather.13.cloned.1.call-update
  16.3 0.0 all-gather.15.cloned.1.call-start
  16.3 0.5 all-gather.15.cloned.1.call-update
  16.8 0.0 all-gather.17.cloned.1.call-start
  16.9 0.5 all-gather.17.cloned.1.call-update
  17.4 10.6 %route.1 = (s32[32,8,128]{2,1,0:T(8,128)}, f32[32,2048]{1,0:T(8,128)}, s32[32,128]{1,0:T(8,128)}) custom-call(s32[8,2048]{1,0:T(8,128)} %bitcast.26, f32[8,2048]{1,0:T(8,128)} %bitcast.27), custom_call_target="tpu_custom_call" | custom-call | flops 10000000000 | bytes 1000000 | tf_op jit(solution)/shard_map/route/pallas_call | solution.py:69
  28.0 1.8 reshape.48.gates_ref
  29.8 1.4 slice_reduce_fusion.count_ref
  31.2 1.0 fusion.2
  32.2 1.3 pad_maximum_fusion.1
  33.5 20.6 %all-gather.9.cloned.1.call-done = bf16[1024,1024]{0,1:T(8,128)(2,1)} async-done(((bf16[1024,64]{0,1:T(8,128)(2,1)}), bf16[1024,1024]{0,1:T(8,128)(2,1)}) %all-gather.9.cloned.1.call-update) | async-done | bytes 2097168 | tf_op jit(solution)/shard_map/all_gather | solution.py:310
  54.2 3.9 copy.27.wout_ref
  58.1 47.3 %all-gather.7.cloned.1.call-done.wqkv_ref = bf16[1024,2048]{1,0:T(8,128)(2,1)} async-done(((bf16[64,2048]{1,0:T(8,128)(2,1)}), bf16[1024,2048]{1,0:T(8,128)(2,1)}) %all-gather.7.cloned.1.call-update) | async-done | bytes 4194320 | tf_op jit(solution)/shard_map/all_gather | solution.py:309
  105.4 80.5 %attention.1 = (f32[16384,128]{1,0:T(8,128)}, f32[16384,128]{1,0:T(8,128)}) custom-call(bf16[4,512,1024]{2,1,0:T(8,128)(2,1)} %x_ref.1, f32[1,1024]{1,0:T(1,128)} %bitcast.28, bf16[1024,2048]{1,0:T(8,128)(2,1)} %all-gather.7.cloned.1.call-done.wqkv_ref, bf16[1024,1024]{1,0:T(8,128)(2,1)} %copy.27.wout_ref, f32[1,1024]{1,0:T(1,128)} %bitcast.29, ...), custom_call_target="tpu_custom_call" | custom-call | flops 60000002048 | bytes 30000000 | tf_op jit(solution)/shard_map/attention/pallas_call | solution.py:158
  185.9 74.6 %all-gather.11.cloned.1.call-done = bf16[32,3,256,512]{3,2,0,1:T(8,128)(2,1)} async-done(((bf16[1,3,256,512]{3,2,0,1:T(8,128)(2,1)}), bf16[32,3,256,512]{3,2,0,1:T(8,128)(2,1)}) %all-gather.11.cloned.1.call-update) | async-done | bytes 25165840 | tf_op jit(solution)/shard_map/all_gather | solution.py:317
  260.5 20.5 %copy.28 = bf16[32,3,256,512]{3,2,1,0:T(8,128)(2,1)} copy(bf16[32,3,256,512]{3,2,0,1:T(8,128)(2,1)} %all-gather.11.cloned.1.call-done) | data formatting | bytes 50331648 | tf_op jit(solution)/shard_map/all_gather | solution.py:317
  281.0 134.2 %all-gather.13.cloned.1.call-done = bf16[32,3,256,512]{3,2,0,1:T(8,128)(2,1)} async-done(((bf16[1,3,256,512]{3,2,0,1:T(8,128)(2,1)}), bf16[32,3,256,512]{3,2,0,1:T(8,128)(2,1)}) %all-gather.13.cloned.1.call-update) | async-done | bytes 25165840 | tf_op jit(solution)/shard_map/all_gather | solution.py:317
  415.3 20.4 %copy.29 = bf16[32,3,256,512]{3,2,1,0:T(8,128)(2,1)} copy(bf16[32,3,256,512]{3,2,0,1:T(8,128)(2,1)} %all-gather.13.cloned.1.call-done) | data formatting | bytes 50331648 | tf_op jit(solution)/shard_map/all_gather | solution.py:317
  435.7 134.3 %all-gather.15.cloned.1.call-done = bf16[32,3,256,512]{3,2,0,1:T(8,128)(2,1)} async-done(((bf16[1,3,256,512]{3,2,0,1:T(8,128)(2,1)}), bf16[32,3,256,512]{3,2,0,1:T(8,128)(2,1)}) %all-gather.15.cloned.1.call-update) | async-done | bytes 25165840 | tf_op jit(solution)/shard_map/all_gather | solution.py:317
  570.0 20.5 %copy.30 = bf16[32,3,256,512]{3,2,1,0:T(8,128)(2,1)} copy(bf16[32,3,256,512]{3,2,0,1:T(8,128)(2,1)} %all-gather.15.cloned.1.call-done) | data formatting | bytes 50331648 | tf_op jit(solution)/shard_map/all_gather | solution.py:317
  590.5 47.5 %experts.4.acc_hbm = f32[16384,128]{1,0:T(8,128)} custom-call(s32[8]{0:T(128)} %constant.45.clone.ids_ref, s32[32]{0:T(128)} %slice_reduce_fusion.count_ref, s32[32,1,1024]{2,1,0:T(1,128)} %bitcast.30, f32[32,1,2048]{2,1,0:T(1,128)} %reshape.48.gates_ref, f32[16384,128]{1,0:T(8,128)} %get-tuple-element.13.z_hbm, ...), custom_call_target="tpu_custom_call", output_to_operand_aliasing={{}: (5, {})} | custom-call | flops 40000000000 | bytes 28000000 | tf_op jit(solution)/shard_map/experts/pallas_call | solution.py:280
  638.0 47.2 %experts.5.acc_hbm = f32[16384,128]{1,0:T(8,128)} custom-call(s32[8]{0:T(128)} %constant.46.clone.ids_ref, s32[32]{0:T(128)} %slice_reduce_fusion.count_ref, s32[32,1,1024]{2,1,0:T(1,128)} %bitcast.31, f32[32,1,2048]{2,1,0:T(1,128)} %reshape.48.gates_ref, f32[16384,128]{1,0:T(8,128)} %get-tuple-element.13.z_hbm, ...), custom_call_target="tpu_custom_call", output_to_operand_aliasing={{}: (5, {})} | custom-call | flops 40000000000 | bytes 28000000 | tf_op jit(solution)/shard_map/experts/pallas_call | solution.py:280
  685.2 46.9 %experts.6.acc_hbm = f32[16384,128]{1,0:T(8,128)} custom-call(s32[8]{0:T(128)} %constant.47.clone.ids_ref, s32[32]{0:T(128)} %slice_reduce_fusion.count_ref, s32[32,1,1024]{2,1,0:T(1,128)} %bitcast.32, f32[32,1,2048]{2,1,0:T(1,128)} %reshape.48.gates_ref, f32[16384,128]{1,0:T(8,128)} %get-tuple-element.13.z_hbm, ...), custom_call_target="tpu_custom_call", output_to_operand_aliasing={{}: (5, {})} | custom-call | flops 40000000000 | bytes 28000000 | tf_op jit(solution)/shard_map/experts/pallas_call | solution.py:280
  732.0 0.0 all-gather.17.cloned.1.call-done
  732.1 20.5 %copy.31 = bf16[32,3,256,512]{3,2,1,0:T(8,128)(2,1)} copy(bf16[32,3,256,512]{3,2,0,1:T(8,128)(2,1)} %all-gather.17.cloned.1.call-done) | data formatting | bytes 50331648 | tf_op jit(solution)/shard_map/all_gather | solution.py:317
  752.6 48.3 %experts.7 = bf16[2048,1024]{1,0:T(8,128)(2,1)} custom-call(s32[8]{0:T(128)} %constant.48.clone.ids_ref, s32[32]{0:T(128)} %slice_reduce_fusion.count_ref, s32[32,1,1024]{2,1,0:T(1,128)} %bitcast.33, f32[32,1,2048]{2,1,0:T(1,128)} %reshape.48.gates_ref, f32[16384,128]{1,0:T(8,128)} %get-tuple-element.13.z_hbm, f32[16384,128]{1,0:T(8,128)} %experts.6.acc_hbm, ...), custom_call_target="tpu_custom_call" | custom-call | flops 40000000000 | bytes 28000000 | tf_op jit(solution)/shard_map/experts/pallas_call | solution.py:280
  (1 shorter events, 0.0 us)
Async XLA Ops:
  6.5 6.3 copy-start
  6.5 47.6 %all-gather.9.cloned.1.call-start = ((), (), s32[]{:S(2)}) async-start(), calls=%async_computation.1 | async-start | bytes 2228224 | tf_op jit(solution)/shard_map/all_gather | solution.py:310
  8.4 96.9 %all-gather.7.cloned.1.call-start = ((), (), s32[]{:S(2)}) async-start(), calls=%async_computation | async-start | bytes 4456448 | tf_op jit(solution)/shard_map/all_gather | solution.py:309
  10.7 249.8 %all-gather.11.cloned.1.call-start = ((), (), s32[]{:S(2)}) async-start(), calls=%async_computation.2 | async-start | bytes 25952256 | tf_op jit(solution)/shard_map/all_gather | solution.py:317
  10.8 2.2 copy-start.1
  15.7 399.6 %all-gather.13.cloned.1.call-start = ((), (), s32[]{:S(2)}) async-start(), calls=%async_computation.3 | async-start | bytes 25952256 | tf_op jit(solution)/shard_map/all_gather | solution.py:317
  16.3 553.8 %all-gather.15.cloned.1.call-start = ((), (), s32[]{:S(2)}) async-start(), calls=%async_computation.4 | async-start | bytes 25952256 | tf_op jit(solution)/shard_map/all_gather | solution.py:317
  16.8 715.2 %all-gather.17.cloned.1.call-start = ((), (), s32[]{:S(2)}) async-start(), calls=%async_computation.5 | async-start | bytes 25952256 | tf_op jit(solution)/shard_map/all_gather | solution.py:317
Sparse Core Ops, SparseCore 0:
  9.5 44.6 all-gather.8
  56.3 48.9 all-gather.6
  108.4 152.0 all-gather.10
  263.4 151.8 all-gather.12
  418.1 151.8 all-gather.14
  572.9 151.8 all-gather.16
